TPU v7x, 32 devices: a whole 2x2x4 slice. The times are simulated.
32 devices in a mesh: gx: 4 (over x, core), gy: 4 (over z), gz: 2 (over y).
Axes of the slice: x: 2, y: 2, z: 4, core: 2. Of those that a mesh axis runs over, the one named last changes fastest.
Arguments:
- columns: int32 [1024, 2048], P(('gx', 'gy', 'gz')), may hold values from 0 to 32767, as said below
- counts: int32 [1024, 2048], P(('gx', 'gy', 'gz')), may hold values from 1 to 63
- nnz_count: int32 [1024], P(('gx', 'gy', 'gz')), may hold values from 1 to 2048, as said below
- selected: int32 [2048], replicated, may hold values from 0 to 32767, as said below
Outputs:
- gene_stats: float32 [2, 32768], P(None, 'gz')
- pca_input: bfloat16 [1024, 2048], P(('gx', 'gy'), 'gz')
Inputs may be any that keep to these rules, and one draw needn't show every extreme that they name: `columns`: in each row no two slots fall in the same block of 16 consecutive genes (so the first nnz_count slots hold distinct genes); slots beyond nnz_count are not part of the matrix. For every k, the live slots of one cell fall on at most 128 of the genes selected[k * 2048 / 2] to selected[(k + 1) * 2048 / 2 - 1]; some cell reaches 128 for every k in every draw. `nnz_count`: some cell has all 2048 slots live in every draw. `selected`: distinct genes.
All inputs are finite; a program needn't handle non-finite values.
Results may differ from a plain program's by a relative error of at most 0.0085.
Values may be sent and summed in bfloat16 or wider, within the bound.
No kernel may reach another device: no remote copies, remote signals or barrier semaphores. Data moves between devices by JAX's collectives and lax.ppermute only.
A program may use at most 128 MiB of HBM per device.

v0:
```python
import jax
import jax.numpy as jnp
from jax import lax
from jax.sharding import PartitionSpec as P

GENES = 32768
SEL = 2048
target_sum = 10000.0
var_floor = 0.01
clip_value = 10.0
lane_count = 256


def standardize(dense, mean_sel, variance_sel):
    scale_sel = jnp.sqrt(jnp.maximum(variance_sel, var_floor))
    return jnp.clip((dense - mean_sel[None, :]) / scale_sel[None, :], -clip_value, clip_value)


def cell_block(pair):
    block_genes, block_values = pair
    high_count = GENES // lane_count
    high_ids = lax.broadcasted_iota(jnp.int32, (1, 1, high_count), 2)
    low_ids = lax.broadcasted_iota(jnp.int32, (1, 1, lane_count), 2)
    high_table = ((block_genes // lane_count)[:, :, None] == high_ids).astype(jnp.bfloat16)
    low_hit = (block_genes % lane_count)[:, :, None] == low_ids
    upper = lax.optimization_barrier(block_values.astype(jnp.bfloat16))
    lower = (block_values - upper.astype(jnp.float32)).astype(jnp.bfloat16)
    upper_table = jnp.where(low_hit, upper[:, :, None], jnp.bfloat16(0.0))
    lower_table = jnp.where(low_hit, lower[:, :, None], jnp.bfloat16(0.0))
    upper_part = jnp.einsum(
        "csh,csl->chl", high_table, upper_table, preferred_element_type=jnp.float32
    )
    lower_part = jnp.einsum(
        "csh,csl->chl", high_table, lower_table, preferred_element_type=jnp.float32
    )
    return upper_part + lower_part


def per_device(columns, counts, nnz_count, selected):
    local_cells = columns.shape[0]
    row_slots = columns.shape[1]
    owners = lax.axis_size("gz")
    owner_index = lax.axis_index("gz")
    cells = local_cells * lax.axis_size("gx") * lax.axis_size("gy") * owners
    slot = lax.broadcasted_iota(jnp.int32, counts.shape, 1)
    live = slot < nnz_count[:, None]
    raw = jnp.where(live, counts.astype(jnp.float32), jnp.float32(0.0))
    library = jnp.sum(raw, axis=1, keepdims=True)
    values = jnp.log1p(raw * (target_sum / library))
    genes = jnp.where(live, columns, 0)
    block_rows = 4
    block_total = local_cells // block_rows
    expanded = lax.map(
        cell_block,
        (
            genes.reshape(block_total, block_rows, row_slots),
            values.reshape(block_total, block_rows, row_slots),
        ),
    )
    expanded = expanded.reshape(local_cells, GENES)
    total = jnp.sum(expanded, axis=0)
    square = jnp.sum(expanded * expanded, axis=0)
    terms = jnp.stack([total, square])
    owned = GENES // owners
    sums = lax.psum(terms, ("gx", "gy", "gz"))
    own_sums = lax.dynamic_slice_in_dim(sums, owner_index * owned, owned, 1)
    picked_sums = jnp.take(sums, selected, axis=1)
    own_mean = own_sums[0] / cells
    own_variance = own_sums[1] / cells - own_mean * own_mean
    gene_stats = jnp.stack([own_mean, own_variance])
    sel_mean = picked_sums[0] / cells
    sel_variance = picked_sums[1] / cells - sel_mean * sel_mean
    dense = jnp.take(expanded, selected, axis=1)
    share_size = SEL // owners
    own_mean_sel = lax.dynamic_slice_in_dim(sel_mean, owner_index * share_size, share_size, 0)
    own_variance_sel = lax.dynamic_slice_in_dim(
        sel_variance, owner_index * share_size, share_size, 0
    )
    moved = lax.all_to_all(
        dense.astype(jnp.bfloat16), "gz", split_axis=1, concat_axis=0, tiled=True
    ).astype(dense.dtype)
    pca_input = standardize(moved, own_mean_sel, own_variance_sel).astype(jnp.bfloat16)
    return (gene_stats, pca_input)


def solution(mesh):
    return jax.shard_map(
        per_device,
        mesh=mesh,
        in_specs=(
            P(("gx", "gy", "gz"), None),
            P(("gx", "gy", "gz"), None),
            P(("gx", "gy", "gz")),
            P(),
        ),
        out_specs=(P(None, "gz"), P(("gx", "gy"), "gz")),
        check_vma=False,
    )
```

profile of v0, /device:TPU:0, one launch (start us, length us, event | category | flops | bytes accessed | tf_op | source)
XLA Modules:
  0.0 230.8 jit_solution(16225255947262282294)
XLA Ops:
  7.2 1.2 fusion.36
  8.4 1.1 multiply_log-plus-one_fusion
  9.5 0.1 reshape.103
  9.6 1.0 fusion.35
  10.7 0.1 reshape.102
  10.8 56.9 %while.12 = (s32[]{:T(128)}, f32[8,4,128,256]{3,2,1,0:T(8,128)}, s32[8,4,2048]{2,1,0:T(4,128)S(1)}, f32[8,4,2048]{2,1,0:T(4,128)S(1)}, s32[]{:T(128)}) while((s32[]{:T(128)}, f32[8,4,128,256]{3,2,1,0:T(8,128)}, s32[8,4,2048]{2,1,0:T(4,128)S(1)}, f32[8,4,2048]{2,1,0:T(4,128)S(1)}, s32[]{:T(128)}) %tuple.39), condition=%wide.region_2.3_spmd, body=%wide.region_1.2_spmd.sunk | while | flops 1084588032 | bytes 1982553 | solution.py:53
  10.8 0.1 add_select_fusion.4
  10.9 3.2 %fusion.48 = f32[4,128,256]{2,1,0:T(8,128)S(1)} fusion(s32[4,2048]{1,0:T(4,128)S(1)} %add_select_fusion.5, bf16[4,2048]{1,0:T(4,128)(2,1)S(1)} %bitcast_convert_fusion.2, s32[4,2048]{1,0:T(4,128)S(1)} %get-tuple-element.109), kind=kOutput, calls=%fused_computation.5.clone.1 | convolution fusion | flops 542113792 | bytes 606208 | tf_op jit(solution)/shard_map/while/body/eval_jaxpr/csh,csl->chl/dot_general | solution.py:30
  14.1 3.8 %fusion.50 = f32[8,4,128,256]{3,2,1,0:T(8,128)} fusion(f32[8,4,128,256]{3,2,1,0:T(8,128)} %get-tuple-element.116, s32[]{:T(128)S(6)} %copy.30, f32[4,128,256]{2,1,0:T(8,128)S(1)} %fusion.48, s32[4,2048]{1,0:T(4,128)S(1)} %add_select_fusion.5, bf16[4,2048]{1,0:T(4,128)(2,1)S(1)} %fusion.49, s32[4,2048]{1,0:T(4,128)S(1)} %get-tuple-element.109), kind=kOutput, calls=%fused_computation.18.clone.1 | convolution fusion | flops 542244864 | bytes 1130500 | tf_op jit(solution)/shard_map/while/body/eval_jaxpr/csh,csl->chl/dot_general | solution.py:33
  17.9 0.1 add_select_fusion.4
  18.0 3.2 %fusion.48 = f32[4,128,256]{2,1,0:T(8,128)S(1)} fusion(s32[4,2048]{1,0:T(4,128)S(1)} %add_select_fusion.5, bf16[4,2048]{1,0:T(4,128)(2,1)S(1)} %bitcast_convert_fusion.2, s32[4,2048]{1,0:T(4,128)S(1)} %get-tuple-element.109), kind=kOutput, calls=%fused_computation.5.clone.1 | convolution fusion | flops 542113792 | bytes 606208 | tf_op jit(solution)/shard_map/while/body/eval_jaxpr/csh,csl->chl/dot_general | solution.py:30
  21.2 3.8 %fusion.50 = f32[8,4,128,256]{3,2,1,0:T(8,128)} fusion(f32[8,4,128,256]{3,2,1,0:T(8,128)} %get-tuple-element.116, s32[]{:T(128)S(6)} %copy.30, f32[4,128,256]{2,1,0:T(8,128)S(1)} %fusion.48, s32[4,2048]{1,0:T(4,128)S(1)} %add_select_fusion.5, bf16[4,2048]{1,0:T(4,128)(2,1)S(1)} %fusion.49, s32[4,2048]{1,0:T(4,128)S(1)} %get-tuple-element.109), kind=kOutput, calls=%fused_computation.18.clone.1 | convolution fusion | flops 542244864 | bytes 1130500 | tf_op jit(solution)/shard_map/while/body/eval_jaxpr/csh,csl->chl/dot_general | solution.py:33
  25.0 0.1 add_select_fusion.4
  25.1 3.2 %fusion.48 = f32[4,128,256]{2,1,0:T(8,128)S(1)} fusion(s32[4,2048]{1,0:T(4,128)S(1)} %add_select_fusion.5, bf16[4,2048]{1,0:T(4,128)(2,1)S(1)} %bitcast_convert_fusion.2, s32[4,2048]{1,0:T(4,128)S(1)} %get-tuple-element.109), kind=kOutput, calls=%fused_computation.5.clone.1 | convolution fusion | flops 542113792 | bytes 606208 | tf_op jit(solution)/shard_map/while/body/eval_jaxpr/csh,csl->chl/dot_general | solution.py:30
  28.3 3.8 %fusion.50 = f32[8,4,128,256]{3,2,1,0:T(8,128)} fusion(f32[8,4,128,256]{3,2,1,0:T(8,128)} %get-tuple-element.116, s32[]{:T(128)S(6)} %copy.30, f32[4,128,256]{2,1,0:T(8,128)S(1)} %fusion.48, s32[4,2048]{1,0:T(4,128)S(1)} %add_select_fusion.5, bf16[4,2048]{1,0:T(4,128)(2,1)S(1)} %fusion.49, s32[4,2048]{1,0:T(4,128)S(1)} %get-tuple-element.109), kind=kOutput, calls=%fused_computation.18.clone.1 | convolution fusion | flops 542244864 | bytes 1130500 | tf_op jit(solution)/shard_map/while/body/eval_jaxpr/csh,csl->chl/dot_general | solution.py:33
  32.1 0.1 add_select_fusion.4
  32.3 3.2 %fusion.48 = f32[4,128,256]{2,1,0:T(8,128)S(1)} fusion(s32[4,2048]{1,0:T(4,128)S(1)} %add_select_fusion.5, bf16[4,2048]{1,0:T(4,128)(2,1)S(1)} %bitcast_convert_fusion.2, s32[4,2048]{1,0:T(4,128)S(1)} %get-tuple-element.109), kind=kOutput, calls=%fused_computation.5.clone.1 | convolution fusion | flops 542113792 | bytes 606208 | tf_op jit(solution)/shard_map/while/body/eval_jaxpr/csh,csl->chl/dot_general | solution.py:30
  35.4 3.8 %fusion.50 = f32[8,4,128,256]{3,2,1,0:T(8,128)} fusion(f32[8,4,128,256]{3,2,1,0:T(8,128)} %get-tuple-element.116, s32[]{:T(128)S(6)} %copy.30, f32[4,128,256]{2,1,0:T(8,128)S(1)} %fusion.48, s32[4,2048]{1,0:T(4,128)S(1)} %add_select_fusion.5, bf16[4,2048]{1,0:T(4,128)(2,1)S(1)} %fusion.49, s32[4,2048]{1,0:T(4,128)S(1)} %get-tuple-element.109), kind=kOutput, calls=%fused_computation.18.clone.1 | convolution fusion | flops 542244864 | bytes 1130500 | tf_op jit(solution)/shard_map/while/body/eval_jaxpr/csh,csl->chl/dot_general | solution.py:33
  39.3 0.1 add_select_fusion.4
  39.4 3.2 %fusion.48 = f32[4,128,256]{2,1,0:T(8,128)S(1)} fusion(s32[4,2048]{1,0:T(4,128)S(1)} %add_select_fusion.5, bf16[4,2048]{1,0:T(4,128)(2,1)S(1)} %bitcast_convert_fusion.2, s32[4,2048]{1,0:T(4,128)S(1)} %get-tuple-element.109), kind=kOutput, calls=%fused_computation.5.clone.1 | convolution fusion | flops 542113792 | bytes 606208 | tf_op jit(solution)/shard_map/while/body/eval_jaxpr/csh,csl->chl/dot_general | solution.py:30
  42.5 3.8 %fusion.50 = f32[8,4,128,256]{3,2,1,0:T(8,128)} fusion(f32[8,4,128,256]{3,2,1,0:T(8,128)} %get-tuple-element.116, s32[]{:T(128)S(6)} %copy.30, f32[4,128,256]{2,1,0:T(8,128)S(1)} %fusion.48, s32[4,2048]{1,0:T(4,128)S(1)} %add_select_fusion.5, bf16[4,2048]{1,0:T(4,128)(2,1)S(1)} %fusion.49, s32[4,2048]{1,0:T(4,128)S(1)} %get-tuple-element.109), kind=kOutput, calls=%fused_computation.18.clone.1 | convolution fusion | flops 542244864 | bytes 1130500 | tf_op jit(solution)/shard_map/while/body/eval_jaxpr/csh,csl->chl/dot_general | solution.py:33
  46.4 0.1 add_select_fusion.4
  46.5 3.2 %fusion.48 = f32[4,128,256]{2,1,0:T(8,128)S(1)} fusion(s32[4,2048]{1,0:T(4,128)S(1)} %add_select_fusion.5, bf16[4,2048]{1,0:T(4,128)(2,1)S(1)} %bitcast_convert_fusion.2, s32[4,2048]{1,0:T(4,128)S(1)} %get-tuple-element.109), kind=kOutput, calls=%fused_computation.5.clone.1 | convolution fusion | flops 542113792 | bytes 606208 | tf_op jit(solution)/shard_map/while/body/eval_jaxpr/csh,csl->chl/dot_general | solution.py:30
  49.6 3.8 %fusion.50 = f32[8,4,128,256]{3,2,1,0:T(8,128)} fusion(f32[8,4,128,256]{3,2,1,0:T(8,128)} %get-tuple-element.116, s32[]{:T(128)S(6)} %copy.30, f32[4,128,256]{2,1,0:T(8,128)S(1)} %fusion.48, s32[4,2048]{1,0:T(4,128)S(1)} %add_select_fusion.5, bf16[4,2048]{1,0:T(4,128)(2,1)S(1)} %fusion.49, s32[4,2048]{1,0:T(4,128)S(1)} %get-tuple-element.109), kind=kOutput, calls=%fused_computation.18.clone.1 | convolution fusion | flops 542244864 | bytes 1130500 | tf_op jit(solution)/shard_map/while/body/eval_jaxpr/csh,csl->chl/dot_general | solution.py:33
  53.5 0.1 add_select_fusion.4
  53.6 3.2 %fusion.48 = f32[4,128,256]{2,1,0:T(8,128)S(1)} fusion(s32[4,2048]{1,0:T(4,128)S(1)} %add_select_fusion.5, bf16[4,2048]{1,0:T(4,128)(2,1)S(1)} %bitcast_convert_fusion.2, s32[4,2048]{1,0:T(4,128)S(1)} %get-tuple-element.109), kind=kOutput, calls=%fused_computation.5.clone.1 | convolution fusion | flops 542113792 | bytes 606208 | tf_op jit(solution)/shard_map/while/body/eval_jaxpr/csh,csl->chl/dot_general | solution.py:30
  56.7 3.8 %fusion.50 = f32[8,4,128,256]{3,2,1,0:T(8,128)} fusion(f32[8,4,128,256]{3,2,1,0:T(8,128)} %get-tuple-element.116, s32[]{:T(128)S(6)} %copy.30, f32[4,128,256]{2,1,0:T(8,128)S(1)} %fusion.48, s32[4,2048]{1,0:T(4,128)S(1)} %add_select_fusion.5, bf16[4,2048]{1,0:T(4,128)(2,1)S(1)} %fusion.49, s32[4,2048]{1,0:T(4,128)S(1)} %get-tuple-element.109), kind=kOutput, calls=%fused_computation.18.clone.1 | convolution fusion | flops 542244864 | bytes 1130500 | tf_op jit(solution)/shard_map/while/body/eval_jaxpr/csh,csl->chl/dot_general | solution.py:33
  60.7 3.2 %fusion.48 = f32[4,128,256]{2,1,0:T(8,128)S(1)} fusion(s32[4,2048]{1,0:T(4,128)S(1)} %add_select_fusion.5, bf16[4,2048]{1,0:T(4,128)(2,1)S(1)} %bitcast_convert_fusion.2, s32[4,2048]{1,0:T(4,128)S(1)} %get-tuple-element.109), kind=kOutput, calls=%fused_computation.5.clone.1 | convolution fusion | flops 542113792 | bytes 606208 | tf_op jit(solution)/shard_map/while/body/eval_jaxpr/csh,csl->chl/dot_general | solution.py:30
  63.8 3.8 %fusion.50 = f32[8,4,128,256]{3,2,1,0:T(8,128)} fusion(f32[8,4,128,256]{3,2,1,0:T(8,128)} %get-tuple-element.116, s32[]{:T(128)S(6)} %copy.30, f32[4,128,256]{2,1,0:T(8,128)S(1)} %fusion.48, s32[4,2048]{1,0:T(4,128)S(1)} %add_select_fusion.5, bf16[4,2048]{1,0:T(4,128)(2,1)S(1)} %fusion.49, s32[4,2048]{1,0:T(4,128)S(1)} %get-tuple-element.109), kind=kOutput, calls=%fused_computation.18.clone.1 | convolution fusion | flops 542244864 | bytes 1130500 | tf_op jit(solution)/shard_map/while/body/eval_jaxpr/csh,csl->chl/dot_general | solution.py:33
  67.7 2.6 %fusion.39 = (f32[128,256]{1,0:T(8,128)S(1)}, f32[128,256]{1,0:T(8,128)S(1)}) fusion(f32[8,4,128,256]{3,2,1,0:T(8,128)} %get-tuple-element.58), kind=kLoop, calls=%fused_computation.62 | loop fusion | flops 3080192 | bytes 4456448 | tf_op jit(solution)/shard_map/reduce_sum | solution.py:61
  70.3 0.1 copy.24
  70.4 0.1 copy.25
  70.6 0.9 pad_maximum_fusion
  71.6 4.4 %copy.26 = bf16[4,8,128,256]{3,1,2,0:T(8,128)(2,1)S(1)} copy(f32[4,8,128,256]{3,2,1,0:T(8,128)} %bitcast.62) | data formatting | bytes 6291456
  76.0 6.0 %copy.21 = bf16[32,32768]{0,1:T(8,128)(2,1)} copy(bf16[32,32768]{1,0:T(8,128)(2,1)S(1)} %bitcast.63) | data formatting | bytes 4194304 | tf_op jit(solution)/shard_map/reshape | solution.py:60
  82.0 10.1 %gather_fusion = bf16[2048,32]{1,0:T(8,128)(2,1)S(1)} fusion(bf16[32,32768]{0,1:T(8,128)(2,1)} %copy.21, s32[2048]{0:T(1024)S(1)} %fusion.38), kind=kCustom, calls=%fused_computation | custom fusion | bytes 270336 | tf_op jit(solution)/shard_map/jit(_take)/gather | solution.py:73
  92.1 0.2 copy.22
  92.3 0.7 select_convert_fusion
  93.0 4.3 %all-to-all-start = ((bf16[32,2,1024]{2,0,1:T(8,128)(2,1)}), bf16[32,2,1024]{2,0,1:T(8,128)(2,1)S(1)}, u32[]{:S(2)}, u32[]{:S(2)}) async-start(bf16[32,2,1024]{2,0,1:T(8,128)(2,1)} %select_convert_fusion), calls=%async_computation | async-start | bytes 262144 | tf_op jit(solution)/shard_map/all_to_all | solution.py:79
  97.3 103.7 %all-reduce.2.cloned.1.call-done = f32[2,32768]{1,0:T(2,128)} async-done(((f32[2,32768]{1,0:T(2,128)}), f32[2,32768]{1,0:T(2,128)}) %all-reduce.2.cloned.1.call-update) | async-done | bytes 262160 | tf_op jit(solution)/shard_map/psum | solution.py:65
  201.0 8.9 %copy.23 = f32[2,32768]{0,1:T(8,128)} copy(f32[2,32768]{1,0:T(2,128)} %all-reduce.2.cloned.1.call-done) | data formatting | bytes 524288 | tf_op jit(solution)/shard_map/psum | solution.py:65
  209.9 11.2 %gather_fusion.1 = f32[2048,2]{1,0:T(8,128)S(1)} fusion(f32[2,32768]{0,1:T(8,128)} %copy.23, s32[2048]{0:T(1024)S(1)} %fusion.38), kind=kCustom, calls=%fused_computation.1 | custom fusion | bytes 40960 | tf_op jit(solution)/shard_map/jit(_take)/gather | solution.py:67
  221.2 0.3 select_bitcast_fusion
  221.5 0.2 dynamic-slice_multiply_fusion.2
  221.7 0.8 pad_maximum_fusion.1
  222.5 0.3 fusion.40
  222.9 0.4 dynamic-slice_reduce_fusion
  223.2 0.7 fusion.34
  (37 shorter events, 0.6 us)
Async XLA Ops:
  7.2 193.8 %all-reduce.2.cloned.1.call-start = ((), (), s32[]{:S(2)}) async-start(), calls=%async_computation.1 | async-start | bytes 524288 | tf_op jit(solution)/shard_map/psum | solution.py:65
  67.7 3.9 %copy-start.1 = (s32[2048]{0:T(1024)S(1)}, s32[2048]{0:T(1024)}, u32[]{:S(2)}) copy-start(s32[2048]{0:T(1024)} %param.9) | copy-start | bytes 24580
  93.0 130.2 %all-to-all-start = ((bf16[32,2,1024]{2,0,1:T(8,128)(2,1)}), bf16[32,2,1024]{2,0,1:T(8,128)(2,1)S(1)}, u32[]{:S(2)}, u32[]{:S(2)}) async-start(bf16[32,2,1024]{2,0,1:T(8,128)(2,1)} %select_convert_fusion), calls=%async_computation | async-start | bytes 262144 | tf_op jit(solution)/shard_map/all_to_all | solution.py:79
  201.0 20.5 %copy-start = (f32[2,32768]{1,0:T(2,128)S(1)}, f32[2,32768]{1,0:T(2,128)}, u32[]{:S(2)}) copy-start(f32[2,32768]{1,0:T(2,128)} %all-reduce.2.cloned.1.call-done) | copy-start | bytes 786436
Sparse Core Ops, SparseCore 0:
  71.7 129.2 all-reduce.1
where the time goes:
time: 231 us
  waiting for transfers between devices  104 us (45%)
  matrix products  55.7 us (24%)
  local copies, waits for them, and re-layouts  41.3 us (18%)
  between operations  14.2 us (6%)
  other arithmetic  11.3 us (5%)
  starting transfers between devices  4.31 us (2%)
    psum x1, waiting for transfers between devices, per_device(): sums = lax.psum(terms, ('gx', 'gy', 'gz'))  104 us
    dot_general x8, matrix products, cell_block(): jnp.einsum('csh,csl->chl', high_table, lower_table, preferred_element_typ...  30.5 us
    dot_general x8, matrix products, cell_block(): jnp.einsum('csh,csl->chl', high_table, upper_table, preferred_element_typ...  25.2 us
    gather x1, local copies, waits for them, and re-layouts, per_device(): picked_sums = jnp.take(sums, selected, axis=1)  11.2 us
    gather x2, local copies, waits for them, and re-layouts, per_device(): dense = jnp.take(expanded, selected, axis=1)  10.3 us
    psum x1, local copies, waits for them, and re-layouts, per_device(): sums = lax.psum(terms, ('gx', 'gy', 'gz'))  8.92 us
    reshape x1, local copies, waits for them, and re-layouts, per_device(): expanded = expanded.reshape(local_cells, GENES)  5.99 us
    unnamed x7, local copies, waits for them, and re-layouts  4.7 us
  transfers between devices with their start and end apart: 2, of which 1 were waited for; matrix products, arithmetic and copies ran while one was open for 19% of the time, Pallas kernels for 0%

commit v1 on v0

--- a/solution.py
+++ b/solution.py
@@ -62,7 +62,7 @@
     square = jnp.sum(expanded * expanded, axis=0)
     terms = jnp.stack([total, square])
     owned = GENES // owners
-    sums = lax.psum(terms, ("gx", "gy", "gz"))
+    sums = jnp.sum(lax.all_gather(terms, ("gx", "gy", "gz")), axis=0)
     own_sums = lax.dynamic_slice_in_dim(sums, owner_index * owned, owned, 1)
     picked_sums = jnp.take(sums, selected, axis=1)
     own_mean = own_sums[0] / cells

time: 231 us -> 187 us (0.81)
  waiting for transfers between devices: 104 us -> 54.2 us
  other arithmetic: 11.3 us -> 17.3 us
    psum x1 -> x0, waiting for transfers between devices: 104 us -> none  [per_device(): sums = lax.psum(terms, ('gx', 'gy', 'gz'))]
    all_gather x0 -> x1, waiting for transfers between devices: none -> 54.2 us  [per_device(): sums = jnp.sum(lax.all_gather(terms, ('gx', 'gy', 'gz')), axis=0)]
    psum x1 -> x0, local copies, waits for them, and re-layouts: 8.92 us -> none  [per_device(): sums = lax.psum(terms, ('gx', 'gy', 'gz'))]
    reduce_sum x0 -> x1, local copies, waits for them, and re-layouts: none -> 8.34 us  [per_device(): sums = jnp.sum(lax.all_gather(terms, ('gx', 'gy', 'gz')), axis=0)]
    reduce_sum x0 -> x1, other arithmetic: none -> 6.1 us  [per_device(): sums = jnp.sum(lax.all_gather(terms, ('gx', 'gy', 'gz')), axis=0)]
    unnamed x7 -> x5, local copies, waits for them, and re-layouts: 4.7 us -> 4.7 us
  transfers between devices with their start and end apart: 2 -> 2, of which waited for: 1 -> 1; matrix products, arithmetic and copies ran while one was open for 19% -> 26% of each run, Pallas kernels for 0% -> 0%
where the time goes in v1:
time: 187 us
  matrix products  55.7 us (30%)
  waiting for transfers between devices  54.2 us (29%)
  local copies, waits for them, and re-layouts  40.9 us (22%)
  other arithmetic  17.3 us (9%)
  between operations  14.1 us (8%)
  starting transfers between devices  4.19 us (2%)
    all_gather x1, waiting for transfers between devices, per_device(): sums = jnp.sum(lax.all_gather(terms, ('gx', 'gy', 'gz')), axis=0)  54.2 us
    dot_general x8, matrix products, cell_block(): jnp.einsum('csh,csl->chl', high_table, lower_table, preferred_element_typ...  30.4 us
    dot_general x8, matrix products, cell_block(): jnp.einsum('csh,csl->chl', high_table, upper_table, preferred_element_typ...  25.2 us
    gather x1, local copies, waits for them, and re-layouts, per_device(): picked_sums = jnp.take(sums, selected, axis=1)  11.2 us
    gather x2, local copies, waits for them, and re-layouts, per_device(): dense = jnp.take(expanded, selected, axis=1)  10.4 us
    reduce_sum x1, local copies, waits for them, and re-layouts, per_device(): sums = jnp.sum(lax.all_gather(terms, ('gx', 'gy', 'gz')), axis=0)  8.34 us
    reduce_sum x1, other arithmetic, per_device(): sums = jnp.sum(lax.all_gather(terms, ('gx', 'gy', 'gz')), axis=0)  6.1 us
    reshape x1, local copies, waits for them, and re-layouts, per_device(): expanded = expanded.reshape(local_cells, GENES)  6.04 us
  transfers between devices with their start and end apart: 2, of which 1 were waited for; matrix products, arithmetic and copies ran while one was open for 26% of the time, Pallas kernels for 0%

profile of v1, /device:TPU:0, one launch (start us, length us, event | category | flops | bytes accessed | tf_op | source)
XLA Modules:
  0.0 186.8 jit_solution(16777828010177647213)
XLA Ops:
  7.2 1.2 fusion.36
  8.4 1.1 multiply_log-plus-one_fusion
  9.5 0.1 reshape.103
  9.6 1.0 fusion.35
  10.7 0.1 reshape.102
  10.8 56.9 %while.12 = (s32[]{:T(128)}, f32[8,4,128,256]{3,2,1,0:T(8,128)}, s32[8,4,2048]{2,1,0:T(4,128)S(1)}, f32[8,4,2048]{2,1,0:T(4,128)S(1)}, s32[]{:T(128)}) while((s32[]{:T(128)}, f32[8,4,128,256]{3,2,1,0:T(8,128)}, s32[8,4,2048]{2,1,0:T(4,128)S(1)}, f32[8,4,2048]{2,1,0:T(4,128)S(1)}, s32[]{:T(128)}) %tuple.39), condition=%wide.region_2.3_spmd, body=%wide.region_1.2_spmd.sunk | while | flops 1084588032 | bytes 1982553 | solution.py:53
  10.8 0.1 add_select_fusion.4
  10.9 3.2 %fusion.48 = f32[4,128,256]{2,1,0:T(8,128)S(1)} fusion(s32[4,2048]{1,0:T(4,128)S(1)} %add_select_fusion.5, bf16[4,2048]{1,0:T(4,128)(2,1)S(1)} %bitcast_convert_fusion.2, s32[4,2048]{1,0:T(4,128)S(1)} %get-tuple-element.109), kind=kOutput, calls=%fused_computation.5.clone.1 | convolution fusion | flops 542113792 | bytes 606208 | tf_op jit(solution)/shard_map/while/body/eval_jaxpr/csh,csl->chl/dot_general | solution.py:30
  14.1 3.8 %fusion.50 = f32[8,4,128,256]{3,2,1,0:T(8,128)} fusion(f32[8,4,128,256]{3,2,1,0:T(8,128)} %get-tuple-element.116, s32[]{:T(128)S(6)} %copy.27, f32[4,128,256]{2,1,0:T(8,128)S(1)} %fusion.48, s32[4,2048]{1,0:T(4,128)S(1)} %add_select_fusion.5, bf16[4,2048]{1,0:T(4,128)(2,1)S(1)} %fusion.49, s32[4,2048]{1,0:T(4,128)S(1)} %get-tuple-element.109), kind=kOutput, calls=%fused_computation.18.clone.1 | convolution fusion | flops 542244864 | bytes 1130500 | tf_op jit(solution)/shard_map/while/body/eval_jaxpr/csh,csl->chl/dot_general | solution.py:33
  17.9 0.1 add_select_fusion.4
  18.0 3.2 %fusion.48 = f32[4,128,256]{2,1,0:T(8,128)S(1)} fusion(s32[4,2048]{1,0:T(4,128)S(1)} %add_select_fusion.5, bf16[4,2048]{1,0:T(4,128)(2,1)S(1)} %bitcast_convert_fusion.2, s32[4,2048]{1,0:T(4,128)S(1)} %get-tuple-element.109), kind=kOutput, calls=%fused_computation.5.clone.1 | convolution fusion | flops 542113792 | bytes 606208 | tf_op jit(solution)/shard_map/while/body/eval_jaxpr/csh,csl->chl/dot_general | solution.py:30
  21.2 3.8 %fusion.50 = f32[8,4,128,256]{3,2,1,0:T(8,128)} fusion(f32[8,4,128,256]{3,2,1,0:T(8,128)} %get-tuple-element.116, s32[]{:T(128)S(6)} %copy.27, f32[4,128,256]{2,1,0:T(8,128)S(1)} %fusion.48, s32[4,2048]{1,0:T(4,128)S(1)} %add_select_fusion.5, bf16[4,2048]{1,0:T(4,128)(2,1)S(1)} %fusion.49, s32[4,2048]{1,0:T(4,128)S(1)} %get-tuple-element.109), kind=kOutput, calls=%fused_computation.18.clone.1 | convolution fusion | flops 542244864 | bytes 1130500 | tf_op jit(solution)/shard_map/while/body/eval_jaxpr/csh,csl->chl/dot_general | solution.py:33
  25.0 0.1 add_select_fusion.4
  25.1 3.2 %fusion.48 = f32[4,128,256]{2,1,0:T(8,128)S(1)} fusion(s32[4,2048]{1,0:T(4,128)S(1)} %add_select_fusion.5, bf16[4,2048]{1,0:T(4,128)(2,1)S(1)} %bitcast_convert_fusion.2, s32[4,2048]{1,0:T(4,128)S(1)} %get-tuple-element.109), kind=kOutput, calls=%fused_computation.5.clone.1 | convolution fusion | flops 542113792 | bytes 606208 | tf_op jit(solution)/shard_map/while/body/eval_jaxpr/csh,csl->chl/dot_general | solution.py:30
  28.3 3.8 %fusion.50 = f32[8,4,128,256]{3,2,1,0:T(8,128)} fusion(f32[8,4,128,256]{3,2,1,0:T(8,128)} %get-tuple-element.116, s32[]{:T(128)S(6)} %copy.27, f32[4,128,256]{2,1,0:T(8,128)S(1)} %fusion.48, s32[4,2048]{1,0:T(4,128)S(1)} %add_select_fusion.5, bf16[4,2048]{1,0:T(4,128)(2,1)S(1)} %fusion.49, s32[4,2048]{1,0:T(4,128)S(1)} %get-tuple-element.109), kind=kOutput, calls=%fused_computation.18.clone.1 | convolution fusion | flops 542244864 | bytes 1130500 | tf_op jit(solution)/shard_map/while/body/eval_jaxpr/csh,csl->chl/dot_general | solution.py:33
  32.1 0.1 add_select_fusion.4
  32.2 3.2 %fusion.48 = f32[4,128,256]{2,1,0:T(8,128)S(1)} fusion(s32[4,2048]{1,0:T(4,128)S(1)} %add_select_fusion.5, bf16[4,2048]{1,0:T(4,128)(2,1)S(1)} %bitcast_convert_fusion.2, s32[4,2048]{1,0:T(4,128)S(1)} %get-tuple-element.109), kind=kOutput, calls=%fused_computation.5.clone.1 | convolution fusion | flops 542113792 | bytes 606208 | tf_op jit(solution)/shard_map/while/body/eval_jaxpr/csh,csl->chl/dot_general | solution.py:30
  35.4 3.8 %fusion.50 = f32[8,4,128,256]{3,2,1,0:T(8,128)} fusion(f32[8,4,128,256]{3,2,1,0:T(8,128)} %get-tuple-element.116, s32[]{:T(128)S(6)} %copy.27, f32[4,128,256]{2,1,0:T(8,128)S(1)} %fusion.48, s32[4,2048]{1,0:T(4,128)S(1)} %add_select_fusion.5, bf16[4,2048]{1,0:T(4,128)(2,1)S(1)} %fusion.49, s32[4,2048]{1,0:T(4,128)S(1)} %get-tuple-element.109), kind=kOutput, calls=%fused_computation.18.clone.1 | convolution fusion | flops 542244864 | bytes 1130500 | tf_op jit(solution)/shard_map/while/body/eval_jaxpr/csh,csl->chl/dot_general | solution.py:33
  39.2 0.1 add_select_fusion.4
  39.3 3.2 %fusion.48 = f32[4,128,256]{2,1,0:T(8,128)S(1)} fusion(s32[4,2048]{1,0:T(4,128)S(1)} %add_select_fusion.5, bf16[4,2048]{1,0:T(4,128)(2,1)S(1)} %bitcast_convert_fusion.2, s32[4,2048]{1,0:T(4,128)S(1)} %get-tuple-element.109), kind=kOutput, calls=%fused_computation.5.clone.1 | convolution fusion | flops 542113792 | bytes 606208 | tf_op jit(solution)/shard_map/while/body/eval_jaxpr/csh,csl->chl/dot_general | solution.py:30
  42.5 3.8 %fusion.50 = f32[8,4,128,256]{3,2,1,0:T(8,128)} fusion(f32[8,4,128,256]{3,2,1,0:T(8,128)} %get-tuple-element.116, s32[]{:T(128)S(6)} %copy.27, f32[4,128,256]{2,1,0:T(8,128)S(1)} %fusion.48, s32[4,2048]{1,0:T(4,128)S(1)} %add_select_fusion.5, bf16[4,2048]{1,0:T(4,128)(2,1)S(1)} %fusion.49, s32[4,2048]{1,0:T(4,128)S(1)} %get-tuple-element.109), kind=kOutput, calls=%fused_computation.18.clone.1 | convolution fusion | flops 542244864 | bytes 1130500 | tf_op jit(solution)/shard_map/while/body/eval_jaxpr/csh,csl->chl/dot_general | solution.py:33
  46.3 0.1 add_select_fusion.4
  46.5 3.2 %fusion.48 = f32[4,128,256]{2,1,0:T(8,128)S(1)} fusion(s32[4,2048]{1,0:T(4,128)S(1)} %add_select_fusion.5, bf16[4,2048]{1,0:T(4,128)(2,1)S(1)} %bitcast_convert_fusion.2, s32[4,2048]{1,0:T(4,128)S(1)} %get-tuple-element.109), kind=kOutput, calls=%fused_computation.5.clone.1 | convolution fusion | flops 542113792 | bytes 606208 | tf_op jit(solution)/shard_map/while/body/eval_jaxpr/csh,csl->chl/dot_general | solution.py:30
  49.6 3.8 %fusion.50 = f32[8,4,128,256]{3,2,1,0:T(8,128)} fusion(f32[8,4,128,256]{3,2,1,0:T(8,128)} %get-tuple-element.116, s32[]{:T(128)S(6)} %copy.27, f32[4,128,256]{2,1,0:T(8,128)S(1)} %fusion.48, s32[4,2048]{1,0:T(4,128)S(1)} %add_select_fusion.5, bf16[4,2048]{1,0:T(4,128)(2,1)S(1)} %fusion.49, s32[4,2048]{1,0:T(4,128)S(1)} %get-tuple-element.109), kind=kOutput, calls=%fused_computation.18.clone.1 | convolution fusion | flops 542244864 | bytes 1130500 | tf_op jit(solution)/shard_map/while/body/eval_jaxpr/csh,csl->chl/dot_general | solution.py:33
  53.5 3.2 %fusion.48 = f32[4,128,256]{2,1,0:T(8,128)S(1)} fusion(s32[4,2048]{1,0:T(4,128)S(1)} %add_select_fusion.5, bf16[4,2048]{1,0:T(4,128)(2,1)S(1)} %bitcast_convert_fusion.2, s32[4,2048]{1,0:T(4,128)S(1)} %get-tuple-element.109), kind=kOutput, calls=%fused_computation.5.clone.1 | convolution fusion | flops 542113792 | bytes 606208 | tf_op jit(solution)/shard_map/while/body/eval_jaxpr/csh,csl->chl/dot_general | solution.py:30
  56.7 3.8 %fusion.50 = f32[8,4,128,256]{3,2,1,0:T(8,128)} fusion(f32[8,4,128,256]{3,2,1,0:T(8,128)} %get-tuple-element.116, s32[]{:T(128)S(6)} %copy.27, f32[4,128,256]{2,1,0:T(8,128)S(1)} %fusion.48, s32[4,2048]{1,0:T(4,128)S(1)} %add_select_fusion.5, bf16[4,2048]{1,0:T(4,128)(2,1)S(1)} %fusion.49, s32[4,2048]{1,0:T(4,128)S(1)} %get-tuple-element.109), kind=kOutput, calls=%fused_computation.18.clone.1 | convolution fusion | flops 542244864 | bytes 1130500 | tf_op jit(solution)/shard_map/while/body/eval_jaxpr/csh,csl->chl/dot_general | solution.py:33
  60.7 3.2 %fusion.48 = f32[4,128,256]{2,1,0:T(8,128)S(1)} fusion(s32[4,2048]{1,0:T(4,128)S(1)} %add_select_fusion.5, bf16[4,2048]{1,0:T(4,128)(2,1)S(1)} %bitcast_convert_fusion.2, s32[4,2048]{1,0:T(4,128)S(1)} %get-tuple-element.109), kind=kOutput, calls=%fused_computation.5.clone.1 | convolution fusion | flops 542113792 | bytes 606208 | tf_op jit(solution)/shard_map/while/body/eval_jaxpr/csh,csl->chl/dot_general | solution.py:30
  63.8 3.8 %fusion.50 = f32[8,4,128,256]{3,2,1,0:T(8,128)} fusion(f32[8,4,128,256]{3,2,1,0:T(8,128)} %get-tuple-element.116, s32[]{:T(128)S(6)} %copy.27, f32[4,128,256]{2,1,0:T(8,128)S(1)} %fusion.48, s32[4,2048]{1,0:T(4,128)S(1)} %add_select_fusion.5, bf16[4,2048]{1,0:T(4,128)(2,1)S(1)} %fusion.49, s32[4,2048]{1,0:T(4,128)S(1)} %get-tuple-element.109), kind=kOutput, calls=%fused_computation.18.clone.1 | convolution fusion | flops 542244864 | bytes 1130500 | tf_op jit(solution)/shard_map/while/body/eval_jaxpr/csh,csl->chl/dot_general | solution.py:33
  67.6 2.6 %fusion.39 = (f32[128,256]{1,0:T(8,128)S(1)}, f32[128,256]{1,0:T(8,128)S(1)}) fusion(f32[8,4,128,256]{3,2,1,0:T(8,128)} %get-tuple-element.58), kind=kLoop, calls=%fused_computation.62 | loop fusion | flops 3080192 | bytes 4456448 | tf_op jit(solution)/shard_map/reduce_sum | solution.py:61
  70.3 0.1 copy.21
  70.4 0.1 copy.22
  70.6 0.9 maximum_bitcast_fusion
  71.6 4.4 %copy.23 = bf16[4,8,128,256]{3,1,2,0:T(8,128)(2,1)S(1)} copy(f32[4,8,128,256]{3,2,1,0:T(8,128)} %bitcast.64) | data formatting | bytes 6291456
  76.0 6.0 %copy.18 = bf16[32,32768]{0,1:T(8,128)(2,1)} copy(bf16[32,32768]{1,0:T(8,128)(2,1)S(1)} %bitcast.65) | data formatting | bytes 4194304 | tf_op jit(solution)/shard_map/reshape | solution.py:60
  82.0 10.2 %gather_fusion = bf16[2048,32]{1,0:T(8,128)(2,1)S(1)} fusion(bf16[32,32768]{0,1:T(8,128)(2,1)} %copy.18, s32[2048]{0:T(1024)S(1)} %fusion.38), kind=kCustom, calls=%fused_computation | custom fusion | bytes 270336 | tf_op jit(solution)/shard_map/jit(_take)/gather | solution.py:73
  92.3 0.2 copy.19
  92.5 0.7 select_convert_fusion
  93.2 4.2 %all-to-all-start = ((bf16[32,2,1024]{2,0,1:T(8,128)(2,1)}), bf16[32,2,1024]{2,0,1:T(8,128)(2,1)S(1)}, u32[]{:S(2)}, u32[]{:S(2)}) async-start(bf16[32,2,1024]{2,0,1:T(8,128)(2,1)} %select_convert_fusion), calls=%async_computation | async-start | bytes 262144 | tf_op jit(solution)/shard_map/all_to_all | solution.py:79
  97.3 54.2 %all-gather.4.cloned.1.call-done = f32[32,2,32768]{2,1,0:T(2,128)} async-done(((f32[1,2,32768]{2,1,0:T(2,128)}), f32[32,2,32768]{2,1,0:T(2,128)}) %all-gather.4.cloned.1.call-update) | async-done | bytes 8388624 | tf_op jit(solution)/shard_map/all_gather | solution.py:65
  151.5 6.1 %reduce_sum.39 = f32[2,32768]{1,0:T(2,128)S(1)} reduce(f32[32,2,32768]{2,1,0:T(2,128)} %all-gather.4.cloned.1.call-done, f32[]{:T(128)} %constant.110.clone.1), dimensions={0}, to_apply=%region_5.6 | reduce | flops 2031616 | bytes 8650756 | tf_op jit(solution)/shard_map/reduce_sum | solution.py:65
  157.6 8.3 %copy.20 = f32[2,32768]{0,1:T(8,128)} copy(f32[2,32768]{1,0:T(2,128)S(1)} %reduce_sum.39) | data formatting | bytes 524288 | tf_op jit(solution)/shard_map/reduce_sum | solution.py:65
  165.9 11.2 %gather_fusion.1 = f32[2048,2]{1,0:T(8,128)S(1)} fusion(f32[2,32768]{0,1:T(8,128)} %copy.20, s32[2048]{0:T(1024)S(1)} %fusion.38), kind=kCustom, calls=%fused_computation.1 | custom fusion | bytes 40960 | tf_op jit(solution)/shard_map/jit(_take)/gather | solution.py:67
  177.2 0.3 select_bitcast_fusion
  177.5 0.2 dynamic-slice_multiply_fusion.2
  177.7 0.8 pad_maximum_fusion
  178.5 0.3 fusion.40
  178.9 0.4 dynamic-slice_reduce_fusion
  179.2 0.7 fusion.34
  (36 shorter events, 0.7 us)
Async XLA Ops:
  7.2 144.3 %all-gather.4.cloned.1.call-start = ((), (), s32[]{:S(2)}) async-start(), calls=%async_computation.1 | async-start | bytes 8650752 | tf_op jit(solution)/shard_map/all_gather | solution.py:65
  67.6 3.9 %copy-start = (s32[2048]{0:T(1024)S(1)}, s32[2048]{0:T(1024)}, u32[]{:S(2)}) copy-start(s32[2048]{0:T(1024)} %param.9) | copy-start | bytes 24580
  93.2 86.1 %all-to-all-start = ((bf16[32,2,1024]{2,0,1:T(8,128)(2,1)}), bf16[32,2,1024]{2,0,1:T(8,128)(2,1)S(1)}, u32[]{:S(2)}, u32[]{:S(2)}) async-start(bf16[32,2,1024]{2,0,1:T(8,128)(2,1)} %select_convert_fusion), calls=%async_computation | async-start | bytes 262144 | tf_op jit(solution)/shard_map/all_to_all | solution.py:79
Sparse Core Ops, SparseCore 0:
  71.7 79.7 all-gather.3
